TPU v7x, 128 devices: a whole 4x4x4 slice. The times are simulated.
128 devices in a mesh: row: 8 (over z, y_hi), col: 16 (over y_lo, x, core).
Axes of the slice: x: 4, y: 4 (y_hi: 2, y_lo: 2; y = y_hi * 2 + y_lo), z: 4, core: 2. Of those that a mesh axis runs over, the one named last changes fastest.
Arguments:
- matrix_tiles: float32 [8, 16, 16, 512, 512], P('row', 'col'), may hold values from -0.25 to 0.25
- tile_rows: int32 [8, 16, 16], P('row', 'col'), may hold values from 0 to 127, as said below
- tile_columns: int32 [8, 16, 16], P('row', 'col'), may hold values from 0 to 63, as said below
- tile_counts: int32 [8, 16], P('row', 'col'), may hold values from 8 to 16, as said below
- primal_iter: float32 [2, 524288], P(None, ('col', 'row')), may hold values from -6 to 6
- dual_iter: float32 [2, 524288], P(None, ('row', 'col')), may hold values from -6 to 6
- requirement: float32 [524288], P('row'), may hold values from -68 to 68
- constraint_kind: int32 [524288], P('row'), may hold values from 0 to 1
- objective: float32 [524288], P('col'), may hold values from -68 to 68
- lower_bound: float32 [524288], P('col'), may hold values from -1.5 to 1.5
- upper_bound: float32 [524288], P('col'), may hold values from -1.5 to 1.5
- variable_kind: int32 [524288], P('col'), may hold values from 0 to 3
Outputs:
- primal_residual: float32 [2, 524288], P(None, ('row', 'col'))
- dual_residual: float32 [2, 524288], P(None, ('col', 'row'))
- metrics: float32 [2, 3], replicated
Inputs may be any that keep to these rules, and one draw needn't show every extreme that they name: `tile_counts`: slots below the count of a list hold live tiles, the others are padding; some list has all 16 slots live. `tile_rows`: in each constraint group, the first (8) slots of its lists name every block row of the group exactly once; later slots name any block row, and repeated tiles add. `tile_columns`: in each variable group, the first (8) slots of its lists name every block column of the group exactly once; later slots name any block column, and repeated tiles add. `constraint_kind`: 0 marks an equality, 1 a constraint of the form at least. `variable_kind`: 0 free, 1 lower bound only, 2 upper bound only, 3 both bounds.
All inputs are finite; a program needn't handle non-finite values.
Results may differ from a plain program's by a relative error of at most 0.0003.
Values sent between devices are 32-bit elements; how exact they have to be, the bound alone decides.
A program may use at most 64 MiB of HBM per device.

v0:
```python
import jax
import jax.numpy as jnp
from jax import lax
from jax.sharding import Mesh
from jax.sharding import PartitionSpec as P

ROW = ("row_0", "row_1")
COL = ("col_0", "col_1", "col_2")
ROW_COL = ("row_0", "row_1", "col_0", "col_1", "col_2")
COL_ROW = ("col_0", "col_1", "col_2", "row_0", "row_1")
HIGHEST_PRECISION = lax.Precision.HIGHEST


def from_everyone(shard, axis):
    copies = jnp.broadcast_to(shard, (lax.axis_size(axis), *shard.shape))
    return lax.all_to_all(copies, axis, split_axis=0, concat_axis=0, tiled=True)


def joined_along(pieces, dim):
    lengths = list(pieces.shape[1:])
    lengths[dim] *= pieces.shape[0]
    return jnp.moveaxis(pieces, 0, dim).reshape(lengths)


def collect(shard, axis, dim):
    pieces = from_everyone(shard, axis)
    return joined_along(pieces, dim)


def cut_along(shard, dim, count):
    lengths = shard.shape
    pieces = shard.reshape(*lengths[:dim], count, lengths[dim] // count, *lengths[dim + 1 :])
    return jnp.moveaxis(pieces, dim, 0)


def sum_at_owner(shard, axis, dim):
    count = lax.axis_size(axis)
    pieces = lax.all_to_all(cut_along(shard, dim, count), axis, 0, 0, tiled=True)
    return jnp.sum(pieces, axis=0)


def one_axis_at_a_time(shard, axes):
    for axis in axes:
        shard = lax.psum(shard, axis)
    return shard


def primal_side(product, require_part, kind_part, dual_part):
    difference = require_part[None, :] - product
    residual = jnp.where(kind_part[None, :] == 1, jnp.maximum(difference, 0.0), difference)
    return (
        residual,
        jnp.sum(residual * residual, axis=1),
        jnp.sum(require_part * require_part),
        jnp.sum(require_part[None, :] * dual_part, axis=1),
    )


def dual_side(transposed, objective, lower_bound, upper_bound, variable_kind, primal_part):
    reduced = objective[None, :] - transposed
    lower_active = (variable_kind == 1) | (variable_kind == 3)
    upper_active = (variable_kind == 2) | (variable_kind == 3)
    multiplier = jnp.where(lower_active[None, :], jnp.maximum(reduced, 0.0), 0.0) + jnp.where(
        upper_active[None, :], jnp.minimum(reduced, 0.0), 0.0
    )
    residual = reduced - multiplier
    bound_sum = jnp.sum(
        lower_bound[None, :] * jnp.maximum(multiplier, 0.0)
        + upper_bound[None, :] * jnp.minimum(multiplier, 0.0),
        axis=1,
    )
    return (
        residual,
        jnp.sum(residual * residual, axis=1),
        jnp.sum(objective * objective),
        jnp.sum(objective[None, :] * primal_part, axis=1),
        bound_sum,
    )


def finish(
    primal_square,
    require_square,
    require_dot,
    dual_square,
    objective_square,
    objective_dot,
    bound_sum,
):
    primal_ratio = jnp.sqrt(primal_square) / (1.0 + jnp.sqrt(require_square))
    dual_ratio = jnp.sqrt(dual_square) / (1.0 + jnp.sqrt(objective_square))
    dual_value = require_dot + bound_sum
    duality_gap = jnp.abs(objective_dot - dual_value) / (
        1.0 + jnp.abs(objective_dot) + jnp.abs(dual_value)
    )
    return jnp.stack([primal_ratio, dual_ratio, duality_gap], axis=1)


def on_device(
    matrix_tiles,
    tile_rows,
    tile_columns,
    tile_counts,
    primal_iter,
    dual_iter,
    requirement,
    constraint_kind,
    objective,
    lower_bound,
    upper_bound,
    variable_kind,
):
    own_tiles = matrix_tiles[0, 0]
    slot_count = own_tiles.shape[0]
    block_size = own_tiles.shape[-1]
    candidates = primal_iter.shape[0]
    active = (lax.iota(jnp.int32, slot_count) < tile_counts[0, 0]).astype(jnp.float32)
    primal_group = collect(primal_iter, ROW, 1)
    dual_group = collect(dual_iter, COL, 1)
    column_blocks = primal_group.shape[1] // block_size
    row_blocks = dual_group.shape[1] // block_size
    column_pick = (
        tile_columns[0, 0][:, None] == lax.iota(jnp.int32, column_blocks)[None, :]
    ).astype(jnp.float32)
    column_pick = column_pick * active[:, None]
    row_pick = (tile_rows[0, 0][:, None] == lax.iota(jnp.int32, row_blocks)[None, :]).astype(
        jnp.float32
    )
    row_pick = row_pick * active[:, None]
    primal_pick = jnp.einsum(
        "tc,scb->stb",
        column_pick,
        primal_group.reshape(candidates, column_blocks, block_size),
        precision=HIGHEST_PRECISION,
    )
    dual_pick = jnp.einsum(
        "tr,srb->stb",
        row_pick,
        dual_group.reshape(candidates, row_blocks, block_size),
        precision=HIGHEST_PRECISION,
    )
    tile_product = jnp.einsum("tij,stj->tsi", own_tiles, primal_pick, precision=HIGHEST_PRECISION)
    tile_transposed = jnp.einsum("tij,sti->tsj", own_tiles, dual_pick, precision=HIGHEST_PRECISION)
    row_share = dual_iter.shape[1]
    column_share = primal_iter.shape[1]
    row_start = lax.axis_index(COL) * row_share
    column_start = lax.axis_index(ROW) * column_share
    product_part = jnp.einsum(
        "tr,tsi->sri", row_pick, tile_product, precision=HIGHEST_PRECISION
    ).reshape(candidates, row_blocks * block_size)
    transposed_part = jnp.einsum(
        "tc,tsj->scj", column_pick, tile_transposed, precision=HIGHEST_PRECISION
    ).reshape(candidates, column_blocks * block_size)
    product = sum_at_owner(product_part, COL, 1)
    transposed = sum_at_owner(transposed_part, ROW, 1)
    require_share = lax.dynamic_slice_in_dim(requirement, row_start, row_share)
    kind_share = lax.dynamic_slice_in_dim(constraint_kind, row_start, row_share)
    primal_residual, primal_square, require_square, require_dot = primal_side(
        product, require_share, kind_share, dual_iter
    )
    objective_share = lax.dynamic_slice_in_dim(objective, column_start, column_share)
    lower_share = lax.dynamic_slice_in_dim(lower_bound, column_start, column_share)
    upper_share = lax.dynamic_slice_in_dim(upper_bound, column_start, column_share)
    variable_share = lax.dynamic_slice_in_dim(variable_kind, column_start, column_share)
    dual_residual, dual_square, objective_square, objective_dot, bound_sum = dual_side(
        transposed, objective_share, lower_share, upper_share, variable_share, primal_iter
    )
    statistics = (
        primal_square,
        require_square,
        require_dot,
        dual_square,
        objective_square,
        objective_dot,
        bound_sum,
    )
    statistics = (
        one_axis_at_a_time(statistics[0], ROW_COL),
        one_axis_at_a_time(statistics[1], ROW_COL),
        one_axis_at_a_time(statistics[2], ROW_COL),
        one_axis_at_a_time(statistics[3], ROW_COL),
        one_axis_at_a_time(statistics[4], ROW_COL),
        one_axis_at_a_time(statistics[5], ROW_COL),
        one_axis_at_a_time(statistics[6], ROW_COL),
    )
    (
        primal_square,
        require_square,
        require_dot,
        dual_square,
        objective_square,
        objective_dot,
        bound_sum,
    ) = statistics
    metrics = finish(
        primal_square,
        require_square,
        require_dot,
        dual_square,
        objective_square,
        objective_dot,
        bound_sum,
    )
    return (primal_residual, dual_residual, metrics)


def solution(mesh):
    torus = Mesh(mesh.devices.reshape(4, 2, 2, 4, 2), ("row_0", "row_1", "col_0", "col_1", "col_2"))
    return jax.shard_map(
        on_device,
        mesh=torus,
        in_specs=(
            P(ROW, COL, None, None, None),
            P(ROW, COL, None),
            P(ROW, COL, None),
            P(ROW, COL),
            P(None, COL_ROW),
            P(None, ROW_COL),
            P(ROW),
            P(ROW),
            P(COL),
            P(COL),
            P(COL),
            P(COL),
        ),
        out_specs=(P(None, ROW_COL), P(None, COL_ROW), P()),
        check_vma=False,
    )
```

profile of v0, /device:TPU:1, one launch (start us, length us, event | category | flops | bytes accessed | tf_op | source)
XLA Modules:
  0.0 119.1 jit_solution(9777826574996980370)
XLA Ops:
  0.6 1.5 %broadcast_in_dim.44 = f32[8,2,4096]{2,1,0:T(2,128)} broadcast(f32[2,4096]{1,0:T(2,128)} %param.16), dimensions={1,2} | broadcast | bytes 294912 | tf_op jit(solution)/shard_map/broadcast_in_dim | solution.py:15
  2.2 8.5 %all-to-all-start = ((f32[8,2,4096]{2,1,0:T(2,128)}), f32[8,2,4096]{2,1,0:T(2,128)S(1)}, u32[]{:S(2)}, u32[]{:S(2)}) async-start(f32[8,2,4096]{2,1,0:T(2,128)} %broadcast_in_dim.44), calls=%async_computation | async-start | bytes 524288 | tf_op jit(solution)/shard_map/all_to_all | solution.py:16
  11.3 0.7 compare_or_fusion.1
  12.0 1.4 %multiply_reduce_fusion.4 = (f32[]{:T(128)}, f32[4096]{0:T(1024)S(1)}, f32[]{:T(128)}, f32[4096]{0:T(1024)S(1)}) fusion(f32[32768]{0:T(1024)} %param.20, s32[]{:T(128)} %select_n.23, f32[65536]{0:T(1024)} %param.18, s32[]{:T(128)S(6)} %select_n.21), kind=kLoop, calls=%fused_computation.21 | loop fusion | flops 16382 | bytes 65552 | tf_op jit(solution)/shard_map/reduce_sum | solution.py:75
  14.2 4.1 %all-to-all-done = f32[8,2,4096]{2,1,0:T(2,128)S(1)} async-done(((f32[8,2,4096]{2,1,0:T(2,128)}), f32[8,2,4096]{2,1,0:T(2,128)S(1)}, u32[]{:S(2)}, u32[]{:S(2)}) %all-to-all-start) | async-done | bytes 262176 | tf_op jit(solution)/shard_map/all_to_all | solution.py:16
  18.3 1.8 %broadcast_in_dim.45 = f32[16,2,4096]{2,1,0:T(2,128)} broadcast(f32[2,4096]{1,0:T(2,128)} %param.17), dimensions={1,2} | broadcast | bytes 557056 | tf_op jit(solution)/shard_map/broadcast_in_dim | solution.py:15
  20.1 6.5 %all-to-all-start.2 = ((f32[16,2,4096]{2,1,0:T(2,128)}), f32[16,2,4096]{2,1,0:T(2,128)S(1)}, u32[]{:S(2)}, u32[]{:S(2)}) async-start(f32[16,2,4096]{2,1,0:T(2,128)} %broadcast_in_dim.45), calls=%async_computation.2 | async-start | bytes 1048576 | tf_op jit(solution)/shard_map/all_to_all | solution.py:16
  26.8 0.9 convolution_bitcast_fusion.2
  27.8 17.2 %fusion.2 = f32[16,2,512]{2,1,0:T(2,128)S(1)} fusion(f32[1,1,16,512,512]{4,3,2,1,0:T(8,128)} %param.12, f32[2,16,512]{2,1,0:T(8,128)S(1)} %convolution_bitcast_fusion.2), kind=kOutput, calls=%fused_computation.2 | convolution fusion | flops 100663296 | bytes 16908288 | tf_op jit(solution)/shard_map/tij,stj->tsi/dot_general | solution.py:142
  45.0 1.0 convolution_bitcast_fusion
  46.4 1.2 %copy.22 = f32[16,2,4096]{2,1,0:T(2,128)} copy(f32[16,2,4096]{2,0,1:T(8,128)S(1)} %bitcast.42) | data formatting | bytes 1048576 | tf_op jit(solution)/shard_map/transpose | solution.py:33
  47.6 5.7 %all-to-all-start.1 = ((f32[16,2,4096]{2,1,0:T(2,128)}), f32[16,2,4096]{2,1,0:T(2,128)S(1)}, u32[]{:S(2)}, u32[]{:S(2)}) async-start(f32[16,2,4096]{2,1,0:T(2,128)} %copy.22), calls=%async_computation.1 | async-start | bytes 1048576 | tf_op jit(solution)/shard_map/all_to_all | solution.py:38
  54.1 11.5 %fusion = f32[16,2,512]{2,1,0:T(2,128)S(1)} fusion(f32[1,1,16,512,512]{4,3,2,1,0:T(8,128)} %param.12, f32[2,16,512]{2,1,0:T(8,128)S(1)} %convolution_bitcast_fusion.3), kind=kOutput, calls=%fused_computation | convolution fusion | flops 100663296 | bytes 16908288 | tf_op jit(solution)/shard_map/tij,sti->tsj/dot_general | solution.py:143
  66.2 0.9 copy.37
  67.1 3.4 %all-to-all-start.3 = ((f32[8,2,4096]{2,1,0:T(2,128)}), f32[8,2,4096]{2,1,0:T(2,128)S(1)}, u32[]{:S(2)}, u32[]{:S(2)}) async-start(f32[8,2,4096]{2,1,0:T(2,128)} %bitcast.39), calls=%async_computation.3 | async-start | bytes 524288 | tf_op jit(solution)/shard_map/all_to_all | solution.py:38
  70.5 0.7 dynamic-slice_compare_fusion
  71.4 0.8 multiply_reduce_fusion.3
  72.2 7.0 %all-to-all-done.3 = f32[8,2,4096]{2,1,0:T(2,128)S(1)} async-done(((f32[8,2,4096]{2,1,0:T(2,128)}), f32[8,2,4096]{2,1,0:T(2,128)S(1)}, u32[]{:S(2)}, u32[]{:S(2)}) %all-to-all-start.3) | async-done | bytes 262176 | tf_op jit(solution)/shard_map/all_to_all | solution.py:38
  79.3 0.9 multiply_reduce_fusion.1
  80.2 7.3 %all-reduce.1 = (f32[2]{0:T(128)S(1)}, f32[2]{0:T(128)S(1)}, f32[2]{0:T(128)S(1)}, f32[]{:T(128)}, f32[2]{0:T(128)S(1)}, /*index=5*/f32[]{:T(128)}) all-reduce(f32[2]{0:T(128)S(1)} %add.119, f32[2]{0:T(128)S(1)} %get-tuple-element.12, ...), channel_id=1, replica_groups=mesh['row_0'=4,'row_1'=2,'col_0'=2,'col_1'=4,'col_2'=2] {'row_0'}, use_global_device_ids=true, to_apply=%region_33.34 | all-reduce | flops 10 | bytes 80 | tf_op jit(solution)/shard_map/psum | solution.py:44
  87.5 5.9 %all-reduce.4 = (f32[2]{0:T(128)S(1)}, f32[2]{0:T(128)S(1)}, f32[2]{0:T(128)S(1)}, f32[]{:T(128)}, f32[2]{0:T(128)S(1)}, /*index=5*/f32[]{:T(128)}) all-reduce(f32[2]{0:T(128)S(1)} %get-tuple-element.20, f32[2]{0:T(128)S(1)} %get-tuple-element.21, ...), channel_id=1, replica_groups=mesh['row_0'=4,'row_1'=2,'col_0'=2,'col_1'=4,'col_2'=2] {'row_1'}, use_global_device_ids=true, to_apply=%region_34.35 | all-reduce | flops 10 | bytes 80 | tf_op jit(solution)/shard_map/psum | solution.py:44
  93.4 4.5 %all-reduce.3 = (f32[2]{0:T(128)S(1)}, f32[2]{0:T(128)S(1)}, f32[2]{0:T(128)S(1)}, f32[]{:T(128)}, f32[2]{0:T(128)S(1)}, /*index=5*/f32[]{:T(128)}) all-reduce(f32[2]{0:T(128)S(1)} %get-tuple-element.38, f32[2]{0:T(128)S(1)} %get-tuple-element.39, ...), channel_id=1, replica_groups=mesh['row_0'=4,'row_1'=2,'col_0'=2,'col_1'=4,'col_2'=2] {'col_0'}, use_global_device_ids=true, to_apply=%region_35.36 | all-reduce | flops 10 | bytes 80 | tf_op jit(solution)/shard_map/psum | solution.py:44
  97.9 8.7 %all-reduce = (f32[2]{0:T(128)S(1)}, f32[2]{0:T(128)S(1)}, f32[2]{0:T(128)S(1)}, f32[]{:T(128)}, f32[2]{0:T(128)S(1)}, /*index=5*/f32[]{:T(128)}) all-reduce(f32[2]{0:T(128)S(1)} %get-tuple-element.32, f32[2]{0:T(128)S(1)} %get-tuple-element.33, ...), channel_id=1, replica_groups=mesh['row_0'=4,'row_1'=2,'col_0'=2,'col_1'=4,'col_2'=2] {'col_1'}, use_global_device_ids=true, to_apply=%region_36.37 | all-reduce | flops 10 | bytes 80 | tf_op jit(solution)/shard_map/psum | solution.py:44
  106.6 10.4 %all-reduce.2 = (f32[2]{0:T(128)S(1)}, f32[2]{0:T(128)S(1)}, f32[2]{0:T(128)S(1)}, f32[]{:T(128)}, f32[2]{0:T(128)S(1)}, /*index=5*/f32[]{:T(128)}) all-reduce(f32[2]{0:T(128)S(1)} %get-tuple-element.14, f32[2]{0:T(128)S(1)} %get-tuple-element.15, ...), channel_id=1, replica_groups=mesh['row_0'=4,'row_1'=2,'col_0'=2,'col_1'=4,'col_2'=2] {'col_2'}, use_global_device_ids=true, to_apply=%region_37.38 | all-reduce | flops 10 | bytes 80 | tf_op jit(solution)/shard_map/psum | solution.py:44
  (33 shorter events, 3.5 us)
Async XLA Ops:
  0.6 44.4 %copy-start.2 = (s32[1,1,16]{2,1,0:T(1,128)S(1)}, s32[1,1,16]{2,1,0:T(1,128)}, u32[]{:S(2)}) copy-start(s32[1,1,16]{2,1,0:T(1,128)} %param.13) | copy-start | bytes 196
  2.2 16.1 %all-to-all-start = ((f32[8,2,4096]{2,1,0:T(2,128)}), f32[8,2,4096]{2,1,0:T(2,128)S(1)}, u32[]{:S(2)}, u32[]{:S(2)}) async-start(f32[8,2,4096]{2,1,0:T(2,128)} %broadcast_in_dim.44), calls=%async_computation | async-start | bytes 524288 | tf_op jit(solution)/shard_map/all_to_all | solution.py:16
  20.1 27.5 %all-to-all-start.2 = ((f32[16,2,4096]{2,1,0:T(2,128)}), f32[16,2,4096]{2,1,0:T(2,128)S(1)}, u32[]{:S(2)}, u32[]{:S(2)}) async-start(f32[16,2,4096]{2,1,0:T(2,128)} %broadcast_in_dim.45), calls=%async_computation.2 | async-start | bytes 1048576 | tf_op jit(solution)/shard_map/all_to_all | solution.py:16
  27.8 37.8 %copy-start.3 = (s32[1,1,16]{2,1,0:T(1,128)S(1)}, s32[1,1,16]{2,1,0:T(1,128)}, u32[]{:S(2)}) copy-start(s32[1,1,16]{2,1,0:T(1,128)} %param.14) | copy-start | bytes 196
  45.0 26.4 %copy-start.1 = (f32[2,4096]{1,0:T(2,128)S(1)}, f32[2,4096]{1,0:T(2,128)}, u32[]{:S(2)}) copy-start(f32[2,4096]{1,0:T(2,128)} %param.17) | copy-start | bytes 98308
  45.0 34.3 %copy-start = (f32[2,4096]{1,0:T(2,128)S(1)}, f32[2,4096]{1,0:T(2,128)}, u32[]{:S(2)}) copy-start(f32[2,4096]{1,0:T(2,128)} %param.16) | copy-start | bytes 98308
  45.0 34.3 %dynamic-slice-start = ((f32[32768]{0:T(1024)}, s32[]{:T(128)}), f32[4096]{0:T(1024)S(1)}, s32[]{:S(2)}) async-start(f32[32768]{0:T(1024)} %param.21, s32[]{:T(128)} %select_n.23), calls=%async_computation.4 | async-start | bytes 33280 | tf_op jit(solution)/shard_map/dynamic_slice | solution.py:162
  45.0 34.3 %dynamic-slice-start.1 = ((f32[32768]{0:T(1024)}, s32[]{:T(128)}), f32[4096]{0:T(1024)S(1)}, s32[]{:S(2)}) async-start(f32[32768]{0:T(1024)} %param.22, s32[]{:T(128)} %select_n.23), calls=%async_computation.5 | async-start | bytes 33280 | tf_op jit(solution)/shard_map/dynamic_slice | solution.py:163
  47.6 19.5 %all-to-all-start.1 = ((f32[16,2,4096]{2,1,0:T(2,128)}), f32[16,2,4096]{2,1,0:T(2,128)S(1)}, u32[]{:S(2)}, u32[]{:S(2)}) async-start(f32[16,2,4096]{2,1,0:T(2,128)} %copy.22), calls=%async_computation.1 | async-start | bytes 1048576 | tf_op jit(solution)/shard_map/all_to_all | solution.py:38
  67.1 12.1 %all-to-all-start.3 = ((f32[8,2,4096]{2,1,0:T(2,128)}), f32[8,2,4096]{2,1,0:T(2,128)S(1)}, u32[]{:S(2)}, u32[]{:S(2)}) async-start(f32[8,2,4096]{2,1,0:T(2,128)} %bitcast.39), calls=%async_computation.3 | async-start | bytes 524288 | tf_op jit(solution)/shard_map/all_to_all | solution.py:38
where the time goes:
time: 120 us; the launch traced here: 119 us
  blocking collectives  36.8 us (31%)
  matrix products  31.5 us (26%)
  starting transfers between devices  24.1 us (20%)
  waiting for transfers between devices  11.1 us (9%)
  local copies, waits for them, and re-layouts  7.04 us (6%)
  other arithmetic  5.56 us (5%)
  between operations  2.92 us (2%)
    psum x5, blocking collectives, one_axis_at_a_time(): shard = lax.psum(shard, axis)  36.8 us
    dot_general x1, matrix products, on_device(): jnp.einsum('tij,stj->tsi', own_tiles, primal_pick, precision=HIGHEST_PREC...  17.2 us
    all_to_all x2, starting transfers between devices, from_everyone(): return lax.all_to_all(copies, axis, split_axis=0, concat_axis=0, tiled=True)  15 us
    dot_general x1, matrix products, on_device(): jnp.einsum('tij,sti->tsj', own_tiles, dual_pick, precision=HIGHEST_PRECIS...  11.5 us
    all_to_all x2, starting transfers between devices, sum_at_owner(): lax.all_to_all(cut_along(shard, dim, count), axis, 0, 0, tiled=True)  9.13 us
    all_to_all x2, waiting for transfers between devices, sum_at_owner(): lax.all_to_all(cut_along(shard, dim, count), axis, 0, 0, tiled=True)  7 us
    all_to_all x2, waiting for transfers between devices, from_everyone(): return lax.all_to_all(copies, axis, split_axis=0, concat_axis=0, tiled=True)  4.11 us
    broadcast_in_dim x2, local copies, waits for them, and re-layouts, from_everyone(): copies = jnp.broadcast_to(shard, (lax.axis_size(axis), *shard.shape))  3.29 us
  transfers between devices with their start and end apart: 4, of which 2 were waited for; matrix products, arithmetic and copies ran while one was open for 33% of the time, Pallas kernels for 0%

commit v1 on v0

--- a/solution.py
+++ b/solution.py
@@ -41,7 +41,8 @@
 
 def one_axis_at_a_time(shard, axes):
     for axis in axes:
-        shard = lax.psum(shard, axis)
+        terms = lax.all_gather(shard, axis, axis=0, tiled=False)
+        shard = terms.sum(axis=0)
     return shard
 
 

time: 120 us -> 151 us (1.26)
  local copies, waits for them, and re-layouts: 7.04 us -> 31.6 us
  other arithmetic: 5.56 us -> 13.4 us
  blocking collectives: 36.8 us -> 32.8 us
  between operations: 2.92 us -> 6.17 us
    psum x5 -> x0, blocking collectives: 36.8 us -> none  [one_axis_at_a_time(): shard = lax.psum(shard, axis)]
    unnamed x0 -> x5, blocking collectives: none -> 32.8 us
    unnamed x9 -> x94, local copies, waits for them, and re-layouts: 0.67 us -> 23.2 us
    reduce_sum x1 -> x37, other arithmetic: 0.86 us -> 8.84 us  [the longest x35 6.65 us: one_axis_at_a_time(): shard = terms.sum(axis=0)]
    all_gather x0 -> x25, local copies, waits for them, and re-layouts: none -> 2.04 us  [one_axis_at_a_time(): terms = lax.all_gather(shard, axis, axis=0, tiled=False)]
  transfers between devices with their start and end apart: 4 -> 4, of which waited for: 2 -> 3; matrix products, arithmetic and copies ran while one was open for 33% -> 21% of each run, Pallas kernels for 0% -> 0%
where the time goes in v1:
time: 151 us; the launch traced here: 150 us
  blocking collectives  32.8 us (22%)
  local copies, waits for them, and re-layouts  31.6 us (21%)
  matrix products  31.5 us (21%)
  starting transfers between devices  24.9 us (16%)
  other arithmetic  13.4 us (9%)
  waiting for transfers between devices  9.74 us (6%)
  between operations  6.17 us (4%)
    unnamed x5, blocking collectives  32.8 us
    unnamed x94, local copies, waits for them, and re-layouts  23.2 us
    dot_general x1, matrix products, on_device(): jnp.einsum('tij,stj->tsi', own_tiles, primal_pick, precision=HIGHEST_PREC...  17.2 us
    all_to_all x2, starting transfers between devices, from_everyone(): return lax.all_to_all(copies, axis, split_axis=0, concat_axis=0, tiled=True)  15 us
    dot_general x1, matrix products, on_device(): jnp.einsum('tij,sti->tsj', own_tiles, dual_pick, precision=HIGHEST_PRECIS...  11.5 us
    all_to_all x2, starting transfers between devices, sum_at_owner(): lax.all_to_all(cut_along(shard, dim, count), axis, 0, 0, tiled=True)  9.89 us
    reduce_sum x35, other arithmetic, one_axis_at_a_time(): shard = terms.sum(axis=0)  6.65 us
    all_to_all x2, waiting for transfers between devices, sum_at_owner(): lax.all_to_all(cut_along(shard, dim, count), axis, 0, 0, tiled=True)  6.15 us
  transfers between devices with their start and end apart: 4, of which 3 were waited for; matrix products, arithmetic and copies ran while one was open for 21% of the time, Pallas kernels for 0%

profile of v1, /device:TPU:1, one launch (start us, length us, event | category | flops | bytes accessed | tf_op | source)
XLA Modules:
  0.0 150.2 jit_solution(17604487044170105821)
XLA Ops:
  0.6 1.5 %broadcast_in_dim.44 = f32[8,2,4096]{2,1,0:T(2,128)} broadcast(f32[2,4096]{1,0:T(2,128)} %param.16), dimensions={1,2} | broadcast | bytes 294912 | tf_op jit(solution)/shard_map/broadcast_in_dim | solution.py:15
  2.2 8.5 %all-to-all-start = ((f32[8,2,4096]{2,1,0:T(2,128)}), f32[8,2,4096]{2,1,0:T(2,128)S(1)}, u32[]{:S(2)}, u32[]{:S(2)}) async-start(f32[8,2,4096]{2,1,0:T(2,128)} %broadcast_in_dim.44), calls=%async_computation | async-start | bytes 524288 | tf_op jit(solution)/shard_map/all_to_all | solution.py:16
  12.0 1.3 multiply_reduce_fusion.4
  13.4 1.3 multiply_reduce_fusion.5
  14.7 3.6 %all-to-all-done = f32[8,2,4096]{2,1,0:T(2,128)S(1)} async-done(((f32[8,2,4096]{2,1,0:T(2,128)}), f32[8,2,4096]{2,1,0:T(2,128)S(1)}, u32[]{:S(2)}, u32[]{:S(2)}) %all-to-all-start) | async-done | bytes 262176 | tf_op jit(solution)/shard_map/all_to_all | solution.py:16
  18.3 1.7 %broadcast_in_dim.45 = f32[16,2,4096]{2,1,0:T(2,128)} broadcast(f32[2,4096]{1,0:T(2,128)} %param.17), dimensions={1,2} | broadcast | bytes 557056 | tf_op jit(solution)/shard_map/broadcast_in_dim | solution.py:15
  20.0 6.5 %all-to-all-start.2 = ((f32[16,2,4096]{2,1,0:T(2,128)}), f32[16,2,4096]{2,1,0:T(2,128)S(1)}, u32[]{:S(2)}, u32[]{:S(2)}) async-start(f32[16,2,4096]{2,1,0:T(2,128)} %broadcast_in_dim.45), calls=%async_computation.2 | async-start | bytes 1048576 | tf_op jit(solution)/shard_map/all_to_all | solution.py:16
  27.7 17.2 %fusion.2 = f32[16,2,512]{2,1,0:T(2,128)S(1)} fusion(f32[1,1,16,512,512]{4,3,2,1,0:T(8,128)} %param.12, f32[2,16,512]{2,1,0:T(8,128)S(1)} %convolution_bitcast_fusion.2), kind=kOutput, calls=%fused_computation.2 | convolution fusion | flops 100663296 | bytes 16908288 | tf_op jit(solution)/shard_map/tij,stj->tsi/dot_general | solution.py:143
  45.9 11.5 %fusion = f32[16,2,512]{2,1,0:T(2,128)S(1)} fusion(f32[1,1,16,512,512]{4,3,2,1,0:T(8,128)} %param.12, f32[2,16,512]{2,1,0:T(8,128)S(1)} %convolution_bitcast_fusion.3), kind=kOutput, calls=%fused_computation | convolution fusion | flops 100663296 | bytes 16908288 | tf_op jit(solution)/shard_map/tij,sti->tsj/dot_general | solution.py:144
  58.8 3.6 %all-to-all-start.3 = ((f32[8,2,4096]{2,1,0:T(2,128)}), f32[8,2,4096]{2,1,0:T(2,128)S(1)}, u32[]{:S(2)}, u32[]{:S(2)}) async-start(f32[8,2,4096]{2,1,0:T(2,128)} %bitcast.59), calls=%async_computation.3 | async-start | bytes 524288 | tf_op jit(solution)/shard_map/all_to_all | solution.py:38
  65.0 6.0 %all-to-all-done.3 = f32[8,2,4096]{2,1,0:T(2,128)S(1)} async-done(((f32[8,2,4096]{2,1,0:T(2,128)}), f32[8,2,4096]{2,1,0:T(2,128)S(1)}, u32[]{:S(2)}, u32[]{:S(2)}) %all-to-all-start.3) | async-done | bytes 262176 | tf_op jit(solution)/shard_map/all_to_all | solution.py:38
  71.0 6.3 %all-to-all-start.1 = ((f32[16,2,4096]{2,1,0:T(2,128)}), f32[16,2,4096]{2,1,0:T(2,128)S(1)}, u32[]{:S(2)}, u32[]{:S(2)}) async-start(f32[16,2,4096]{2,1,0:T(2,128)} %copy.22), calls=%async_computation.1 | async-start | bytes 1048576 | tf_op jit(solution)/shard_map/all_to_all | solution.py:38
  81.6 1.3 dynamic-update-slice.5
  88.8 6.5 %all-reduce.36 = (f32[8]{0:T(128)S(1)}, f32[8]{0:T(128)S(1)}, f32[8]{0:T(128)S(1)}, f32[8]{0:T(128)S(1)}, f32[4]{0:T(128)S(1)}, /*index=5*/f32[8]{0:T(128)S(1)}, f32[4]{0:T(128)S(1)}) all-reduce(f32[8]{0:T(128)S(1)} %dynamic-update-slice.20, ...), channel_id=12, replica_groups=mesh['row_0'=4,'row_1'=2,'col_0'=2,'col_1'=4,'col_2'=2] {'row_0'}, use_global_device_ids=true, to_apply=%add.20 | all-reduce | flops 48 | bytes 384
  98.3 1.4 dynamic-update-slice.16
  101.7 5.3 %all-reduce.39 = (f32[4]{0:T(128)S(1)}, f32[4]{0:T(128)S(1)}, f32[4]{0:T(128)S(1)}, f32[4]{0:T(128)S(1)}, f32[2]{0:T(128)S(1)}, /*index=5*/f32[4]{0:T(128)S(1)}, f32[2]{0:T(128)S(1)}) all-reduce(f32[4]{0:T(128)S(1)} %dynamic-update-slice.21, ...), channel_id=13, replica_groups=mesh['row_0'=4,'row_1'=2,'col_0'=2,'col_1'=4,'col_2'=2] {'row_1'}, use_global_device_ids=true, to_apply=%add.21 | all-reduce | flops 24 | bytes 192
  109.6 1.3 dynamic-update-slice.17
  113.1 3.8 %all-reduce.38 = (f32[4]{0:T(128)S(1)}, f32[4]{0:T(128)S(1)}, f32[4]{0:T(128)S(1)}, f32[4]{0:T(128)S(1)}, f32[2]{0:T(128)S(1)}, /*index=5*/f32[4]{0:T(128)S(1)}, f32[2]{0:T(128)S(1)}) all-reduce(f32[4]{0:T(128)S(1)} %dynamic-update-slice.22, ...), channel_id=14, replica_groups=mesh['row_0'=4,'row_1'=2,'col_0'=2,'col_1'=4,'col_2'=2] {'col_0'}, use_global_device_ids=true, to_apply=%add.22 | all-reduce | flops 24 | bytes 192
  119.6 1.4 dynamic-update-slice.18
  121.0 1.4 dynamic-update-slice.8
  123.3 8.4 %all-reduce.35 = (f32[8]{0:T(128)S(1)}, f32[8]{0:T(128)S(1)}, f32[8]{0:T(128)S(1)}, f32[8]{0:T(128)S(1)}, f32[4]{0:T(128)S(1)}, /*index=5*/f32[8]{0:T(128)S(1)}, f32[4]{0:T(128)S(1)}) all-reduce(f32[8]{0:T(128)S(1)} %dynamic-update-slice.23, ...), channel_id=15, replica_groups=mesh['row_0'=4,'row_1'=2,'col_0'=2,'col_1'=4,'col_2'=2] {'col_1'}, use_global_device_ids=true, to_apply=%add.23 | all-reduce | flops 48 | bytes 384
  134.7 1.4 dynamic-update-slice.19
  136.2 1.4 dynamic-update-slice.9
  137.5 8.8 %all-reduce.37 = (f32[4]{0:T(128)S(1)}, f32[4]{0:T(128)S(1)}, f32[4]{0:T(128)S(1)}, f32[4]{0:T(128)S(1)}, f32[2]{0:T(128)S(1)}, /*index=5*/f32[4]{0:T(128)S(1)}, f32[2]{0:T(128)S(1)}) all-reduce(f32[4]{0:T(128)S(1)} %dynamic-update-slice.24, ...), channel_id=16, replica_groups=mesh['row_0'=4,'row_1'=2,'col_0'=2,'col_1'=4,'col_2'=2] {'col_2'}, use_global_device_ids=true, to_apply=%add.24 | all-reduce | flops 24 | bytes 192
  (177 shorter events, 32.4 us)
Async XLA Ops:
  0.6 44.9 %copy-start.3 = (s32[1,1,16]{2,1,0:T(1,128)S(1)}, s32[1,1,16]{2,1,0:T(1,128)}, u32[]{:S(2)}) copy-start(s32[1,1,16]{2,1,0:T(1,128)} %param.13) | copy-start | bytes 196
  2.2 16.1 %all-to-all-start = ((f32[8,2,4096]{2,1,0:T(2,128)}), f32[8,2,4096]{2,1,0:T(2,128)S(1)}, u32[]{:S(2)}, u32[]{:S(2)}) async-start(f32[8,2,4096]{2,1,0:T(2,128)} %broadcast_in_dim.44), calls=%async_computation | async-start | bytes 524288 | tf_op jit(solution)/shard_map/all_to_all | solution.py:16
  20.0 25.0 %all-to-all-start.2 = ((f32[16,2,4096]{2,1,0:T(2,128)}), f32[16,2,4096]{2,1,0:T(2,128)S(1)}, u32[]{:S(2)}, u32[]{:S(2)}) async-start(f32[16,2,4096]{2,1,0:T(2,128)} %broadcast_in_dim.45), calls=%async_computation.2 | async-start | bytes 1048576 | tf_op jit(solution)/shard_map/all_to_all | solution.py:16
  27.7 29.6 %copy-start.2 = (s32[1,1,16]{2,1,0:T(1,128)S(1)}, s32[1,1,16]{2,1,0:T(1,128)}, u32[]{:S(2)}) copy-start(s32[1,1,16]{2,1,0:T(1,128)} %param.14) | copy-start | bytes 196
  44.9 33.0 %copy-start.8 = (u32[128]{0:T(128)S(1)}, u32[128]{0:T(128)}, u32[]{:S(2)}) copy-start(u32[128]{0:T(128)} %constant.51) | copy-start | bytes 1540
  44.9 33.6 %copy-start.7 = (u32[128]{0:T(128)S(1)}, u32[128]{0:T(128)}, u32[]{:S(2)}) copy-start(u32[128]{0:T(128)} %constant.56) | copy-start | bytes 1540
  45.0 35.5 %copy-start.6 = (u32[128]{0:T(128)S(1)}, u32[128]{0:T(128)}, u32[]{:S(2)}) copy-start(u32[128]{0:T(128)} %constant.61) | copy-start | bytes 1540
  45.0 40.1 %copy-start = (f32[2,4096]{1,0:T(2,128)S(1)}, f32[2,4096]{1,0:T(2,128)}, u32[]{:S(2)}) copy-start(f32[2,4096]{1,0:T(2,128)} %param.16) | copy-start | bytes 98308
  45.0 40.1 %dynamic-slice-start = ((f32[32768]{0:T(1024)}, s32[]{:T(128)}), f32[4096]{0:T(1024)S(1)}, s32[]{:S(2)}) async-start(f32[32768]{0:T(1024)} %param.21, s32[]{:T(128)} %select_n.23), calls=%async_computation.4 | async-start | bytes 33280 | tf_op jit(solution)/shard_map/dynamic_slice | solution.py:163
  45.0 40.0 %dynamic-slice-start.1 = ((f32[32768]{0:T(1024)}, s32[]{:T(128)}), f32[4096]{0:T(1024)S(1)}, s32[]{:S(2)}) async-start(f32[32768]{0:T(1024)} %param.22, s32[]{:T(128)} %select_n.23), calls=%async_computation.5 | async-start | bytes 33280 | tf_op jit(solution)/shard_map/dynamic_slice | solution.py:164
  45.0 41.9 %copy-start.1 = (f32[2,4096]{1,0:T(2,128)S(1)}, f32[2,4096]{1,0:T(2,128)}, u32[]{:S(2)}) copy-start(f32[2,4096]{1,0:T(2,128)} %param.17) | copy-start | bytes 98308
  45.0 43.2 %copy-start.5 = (u32[128]{0:T(128)S(1)}, u32[128]{0:T(128)}, u32[]{:S(2)}) copy-start(u32[128]{0:T(128)} %constant.66) | copy-start | bytes 1540
  45.0 67.5 %copy-start.4 = (u32[128]{0:T(128)S(1)}, u32[128]{0:T(128)}, u32[]{:S(2)}) copy-start(u32[128]{0:T(128)} %constant.71) | copy-start | bytes 1540
  58.8 12.1 %all-to-all-start.3 = ((f32[8,2,4096]{2,1,0:T(2,128)}), f32[8,2,4096]{2,1,0:T(2,128)S(1)}, u32[]{:S(2)}, u32[]{:S(2)}) async-start(f32[8,2,4096]{2,1,0:T(2,128)} %bitcast.59), calls=%async_computation.3 | async-start | bytes 524288 | tf_op jit(solution)/shard_map/all_to_all | solution.py:38
  71.0 15.8 %all-to-all-start.1 = ((f32[16,2,4096]{2,1,0:T(2,128)}), f32[16,2,4096]{2,1,0:T(2,128)S(1)}, u32[]{:S(2)}, u32[]{:S(2)}) async-start(f32[16,2,4096]{2,1,0:T(2,128)} %copy.22), calls=%async_computation.1 | async-start | bytes 1048576 | tf_op jit(solution)/shard_map/all_to_all | solution.py:38
